TPU v7x, 32 devices: a whole 2x2x4 slice. The times are simulated.
32 devices in a mesh: seq: 8 (over z, x), head: 4 (over y, core).
Axes of the slice: x: 2, y: 2, z: 4, core: 2. Of those that a mesh axis runs over, the one named last changes fastest.
Arguments:
- patches: bfloat16 [32768, 768], P('seq'), may hold values from -6 to 6
- slot_image: int32 [128], P('seq'), may hold values from -1 to 63, as said below
- slot_dest: int32 [128], P('seq'), may hold values from -1 to 63, as said below
- enc_gain: float32 [768], replicated, may hold values from 0.1 to 1.9
- w_qkv: bfloat16 [3, 768, 768], P(None, None, 'head'), may hold values from -1.2 to 1.2
- w_out: bfloat16 [768, 768], P('head'), may hold values from -0.21875 to 0.21875
- fast_gain: float32 [768], replicated, may hold values from 0.1 to 1.9
- w_fast: bfloat16 [3, 768, 768], P(None, None, 'head'), may hold values from -0.21875 to 0.21875
- w_rate: bfloat16 [768, 4], P(None, 'head'), may hold values from -0.21875 to 0.21875
- fast_gate_up: float32 [4, 2, 192, 384], P('head'), may hold values from -0.4375 to 0.4375
- fast_down: float32 [4, 384, 192], P('head'), may hold values from -0.3125 to 0.3125
Outputs:
- view_out: bfloat16 [16384, 768], P('seq', 'head')
Inputs may be any that keep to these rules, and one draw needn't show every extreme that they name: slot_dest gives for each slot the view-order block that its block becomes, or -1 for an empty slot; every view-order block is named by exactly one slot. Slots 2i and 2i + 1 of one seq index are both empty or name view blocks 2m and 2m + 1. The slots of one seq index name at most 2 blocks of any one view shard (blocks s * 8 to (s + 1) * 8 - 1), and some seq index uses all of its slots. slot_image is -1 exactly where slot_dest is -1; an image is one block or the two blocks of a slot pair, and different images have different ids.
All inputs are finite; a program needn't handle non-finite values.
Results may differ from a plain program's by a relative error of at most 0.035.
Values may be sent and summed in bfloat16 or wider, within the bound.
A program may use at most 128 MiB of HBM per device.

v0:
```python
import jax
import jax.numpy as jnp
from jax import lax
from jax.sharding import PartitionSpec as P

HDIM = 64
BLK = 256
BLK_DEV = 8
EPSILON = 1e-06
RATE_SCALE = 0.1


def norm_rows(values, gain_vector):
    widened = values.astype(jnp.float32)
    factor = lax.rsqrt(jnp.mean(widened * widened, axis=-1, keepdims=True) + EPSILON)
    return (widened * factor * gain_vector).astype(jnp.bfloat16)


def attend_pair(pieces):
    query_rows, key_rows, value_rows, token_ids = pieces
    token_count = query_rows.shape[0]
    heads_here = query_rows.shape[1] // HDIM
    q_heads = query_rows.reshape(token_count, heads_here, HDIM)
    k_heads = key_rows.reshape(token_count, heads_here, HDIM)
    v_heads = value_rows.reshape(token_count, heads_here, HDIM)
    scores = jnp.einsum(
        "qhe,khe->hqk", q_heads, k_heads, preferred_element_type=jnp.float32
    ) * HDIM ** (-0.5)
    allowed = token_ids[:, None] == token_ids[None, :]
    scores = jnp.where(allowed[None], scores, -1e30)
    top_score = jnp.max(scores, axis=-1, keepdims=True)
    exp_scores = jnp.exp(scores - top_score)
    weights = (exp_scores / jnp.sum(exp_scores, axis=-1, keepdims=True)).astype(jnp.bfloat16)
    mixed_heads = jnp.einsum("hqk,khe->qhe", weights, v_heads, preferred_element_type=jnp.float32)
    return mixed_heads.astype(jnp.bfloat16).reshape(token_count, heads_here * HDIM)


def encode_blocks(full_rows, block_ids, enc_gain, w_qkv):
    normed = norm_rows(full_rows, enc_gain)
    query_rows = jnp.dot(normed, w_qkv[0], preferred_element_type=jnp.float32).astype(jnp.bfloat16)
    key_rows = jnp.dot(normed, w_qkv[1], preferred_element_type=jnp.float32).astype(jnp.bfloat16)
    value_rows = jnp.dot(normed, w_qkv[2], preferred_element_type=jnp.float32).astype(jnp.bfloat16)
    columns = query_rows.shape[1]
    span = 2 * BLK
    pair_count = full_rows.shape[0] // span
    token_ids = jnp.repeat(block_ids, BLK, total_repeat_length=pair_count * span).reshape(
        pair_count, span
    )
    attended = lax.map(
        attend_pair,
        (
            query_rows.reshape(pair_count, span, columns),
            key_rows.reshape(pair_count, span, columns),
            value_rows.reshape(pair_count, span, columns),
            token_ids,
        ),
    )
    return attended.reshape(pair_count * span, columns)


def route_matrix(destinations, seq_count, room):
    slot_count = destinations.shape[0]
    target_seq = jnp.where(destinations >= 0, destinations // BLK_DEV, -1)
    position = jnp.arange(slot_count)
    earlier = position[None, :] < position[:, None]
    same_target = (target_seq[None, :] == target_seq[:, None]) & earlier
    ranking = jnp.sum(same_target.astype(jnp.int32), axis=1)
    bucket = jnp.where(destinations >= 0, target_seq * room + ranking, -1)
    return bucket[None, :] == jnp.arange(seq_count * room)[:, None]


def pack_rows(selection, payload):
    return jnp.dot(
        selection.astype(jnp.bfloat16), payload, preferred_element_type=jnp.float32
    ).astype(jnp.bfloat16)


def pack_index(selection, indices):
    return jnp.sum(jnp.where(selection, indices[None, :] + 1, 0), axis=1).astype(jnp.int32) - 1


def place_matrix(arrived, seq_index):
    local_block = arrived - seq_index * BLK_DEV
    return (local_block[None, :] == jnp.arange(BLK_DEV)[:, None]) & (arrived >= 0)[None, :]


def renorm(updated, initial):
    target_norm = jnp.sqrt(jnp.sum(initial * initial, axis=1, keepdims=True))
    return (
        updated
        * target_norm
        * lax.rsqrt(jnp.sum(updated * updated, axis=1, keepdims=True) + EPSILON)
    )


def on_device(
    patches,
    slot_image,
    slot_dest,
    enc_gain,
    w_qkv,
    w_out,
    fast_gain,
    w_fast,
    w_rate,
    fast_gate_up,
    fast_down,
):
    seq_count = lax.axis_size("seq")
    seq_index = lax.axis_index("seq")
    head_index = lax.axis_index("head")
    width = w_out.shape[0]
    slot_count = slot_dest.shape[0]
    room = 2 * ((BLK_DEV + seq_count - 1) // seq_count)
    patch_blocks = patches.reshape(slot_count, BLK, patches.shape[1])
    own_columns = lax.dynamic_slice_in_dim(patch_blocks, head_index * width, width, 2).reshape(
        slot_count, BLK * width
    )
    selection = route_matrix(slot_dest, seq_count, room)
    sent_dest = pack_index(selection, slot_dest)
    got_own, arrived, got_ids = (
        lax.all_to_all(
            pack_rows(selection, own_columns), "seq", split_axis=0, concat_axis=0, tiled=True
        ),
        lax.all_to_all(sent_dest, "seq", split_axis=0, concat_axis=0, tiled=True),
        lax.all_to_all(
            pack_index(selection, slot_image), "seq", split_axis=0, concat_axis=0, tiled=True
        ),
    )
    placing = place_matrix(arrived, seq_index)
    view_own = pack_rows(placing, got_own)
    view_ids = pack_index(placing, got_ids)
    whole_rows = lax.all_gather(view_own.reshape(BLK_DEV * BLK, width), "head", axis=1, tiled=True)
    view_attn = encode_blocks(whole_rows, view_ids, enc_gain, w_qkv)
    partial_value = jnp.dot(view_attn, w_out, preferred_element_type=jnp.float32)
    head_mixed = lax.psum_scatter(
        partial_value.astype(jnp.bfloat16), "head", scatter_dimension=1, tiled=True
    ).astype(jnp.float32)
    embedded = (head_mixed + view_own.reshape(BLK_DEV * BLK, width).astype(jnp.float32)).astype(
        jnp.bfloat16
    )
    full_embedded = lax.all_gather(embedded, "head", axis=1, tiled=True)
    normed_fast = norm_rows(full_embedded, fast_gain)
    fast_query = jnp.dot(normed_fast, w_fast[0], preferred_element_type=jnp.float32).astype(
        jnp.bfloat16
    )
    fast_key = jnp.dot(normed_fast, w_fast[1], preferred_element_type=jnp.float32).astype(
        jnp.bfloat16
    )
    fast_value = jnp.dot(normed_fast, w_fast[2], preferred_element_type=jnp.float32).astype(
        jnp.bfloat16
    )
    token_total = embedded.shape[0] * seq_count
    rates = (
        RATE_SCALE
        * jax.nn.softplus(jnp.dot(normed_fast, w_rate, preferred_element_type=jnp.float32))
        * token_total ** (-0.5)
    )
    gate_init = fast_gate_up[0, 0]
    up_init = fast_gate_up[0, 1]
    down_init = fast_down[0]
    gate_half = gate_init.astype(jnp.bfloat16)
    up_half = up_init.astype(jnp.bfloat16)
    down_half = down_init.astype(jnp.bfloat16)
    key_gate = jnp.dot(fast_key, gate_half, preferred_element_type=jnp.float32)
    key_up = jnp.dot(fast_key, up_half, preferred_element_type=jnp.float32)
    hidden_key = (jax.nn.silu(key_gate) * key_up).astype(jnp.bfloat16)
    out_grad = (-rates * fast_value.astype(jnp.float32)).astype(jnp.bfloat16)
    grad_down = jnp.einsum("th,tf->hf", hidden_key, out_grad, preferred_element_type=jnp.float32)
    hidden_grad = jnp.dot(out_grad, down_half.T, preferred_element_type=jnp.float32)
    sigmoid_gate = jax.nn.sigmoid(key_gate)
    gate_grad = (
        hidden_grad * key_up * sigmoid_gate * (1.0 + key_gate * (1.0 - sigmoid_gate))
    ).astype(jnp.bfloat16)
    up_grad = (hidden_grad * jax.nn.silu(key_gate)).astype(jnp.bfloat16)
    grad_gate = jnp.einsum("tf,th->fh", fast_key, gate_grad, preferred_element_type=jnp.float32)
    grad_up = jnp.einsum("tf,th->fh", fast_key, up_grad, preferred_element_type=jnp.float32)
    grad_gate, grad_up, grad_down = (
        lax.psum(grad_gate.astype(jnp.bfloat16), "seq").astype(jnp.float32),
        lax.psum(grad_up.astype(jnp.bfloat16), "seq").astype(jnp.float32),
        lax.psum(grad_down.astype(jnp.bfloat16), "seq").astype(jnp.float32),
    )
    new_gate = renorm(gate_init - grad_gate, gate_init)
    new_up = renorm(up_init - grad_up, up_init)
    new_down = renorm(down_init - grad_down, down_init)
    applied_gate = new_gate.astype(jnp.bfloat16)
    applied_up = new_up.astype(jnp.bfloat16)
    applied_down = new_down.astype(jnp.bfloat16)
    query_gate = jnp.dot(fast_query, applied_gate, preferred_element_type=jnp.float32)
    query_up = jnp.dot(fast_query, applied_up, preferred_element_type=jnp.float32)
    query_hidden = (jax.nn.silu(query_gate) * query_up).astype(jnp.bfloat16)
    fast_out = jnp.dot(query_hidden, applied_down, preferred_element_type=jnp.float32)
    return (embedded.astype(jnp.float32) + fast_out).astype(jnp.bfloat16)


def solution(mesh):
    in_specs = (
        P("seq", None),
        P("seq"),
        P("seq"),
        P(),
        P(None, None, "head"),
        P("head", None),
        P(),
        P(None, None, "head"),
        P(None, "head"),
        P("head", None, None, None),
        P("head", None, None),
    )
    out_specs = P("seq", "head")
    return jax.shard_map(
        on_device, mesh=mesh, in_specs=in_specs, out_specs=out_specs, check_vma=False
    )
```

profile of v0, /device:TPU:0, one launch (start us, length us, event | category | flops | bytes accessed | tf_op | source)
XLA Modules:
  0.0 311.4 jit_solution(212847610619158784)
XLA Ops:
  9.6 7.3 %all-to-all-start = ((s32[8,2,1]{1,2,0:T(1,128)}), s32[8,2,1]{1,2,0:T(1,128)S(1)}, u32[]{:S(2)}, u32[]{:S(2)}) async-start(s32[8,2,1]{1,2,0:T(1,128)} %bitcast.6), calls=%async_computation | async-start | bytes 8192 | tf_op jit(solution)/shard_map/all_to_all | solution.py:125
  16.8 2.9 constant_dynamic-slice_fusion.4
  19.8 3.2 %reshape.274 = bf16[16,49152]{1,0:T(8,128)(2,1)} reshape(bf16[16,256,192]{2,1,0:T(8,128)(2,1)S(1)} %constant_dynamic-slice_fusion.4) | data formatting | bytes 3145728 | tf_op jit(solution)/shard_map/reshape | solution.py:116
  23.0 2.0 convolution_convert_fusion
  24.9 1.9 all_to_all.17
  26.9 6.0 %all-to-all-start.1 = ((bf16[8,2,49152]{2,1,0:T(2,128)(2,1)}), bf16[8,2,49152]{2,1,0:T(2,128)(2,1)S(1)}, u32[]{:S(2)}, u32[]{:S(2)}) async-start(bf16[8,2,49152]{2,1,0:T(2,128)(2,1)} %all_to_all.17), calls=%async_computation.1 | async-start | bytes 3145728 | tf_op jit(solution)/shard_map/all_to_all | solution.py:122
  33.1 36.2 %all-to-all-done.1 = bf16[8,2,49152]{2,1,0:T(2,128)(2,1)S(1)} async-done(((bf16[8,2,49152]{2,1,0:T(2,128)(2,1)}), bf16[8,2,49152]{2,1,0:T(2,128)(2,1)S(1)}, u32[]{:S(2)}, u32[]{:S(2)}) %all-to-all-start.1) | async-done | bytes 1572896 | tf_op jit(solution)/shard_map/all_to_all | solution.py:122
  70.0 1.2 convolution_convert_fusion.1
  71.3 2.3 reshape.275
  73.6 1.2 copy.34
  75.5 3.6 %all-to-all-start.2 = ((s32[8,2,1]{1,2,0:T(1,128)}), s32[8,2,1]{1,2,0:T(1,128)S(1)}, u32[]{:S(2)}, u32[]{:S(2)}) async-start(s32[8,2,1]{1,2,0:T(1,128)} %bitcast.9), calls=%async_computation.2 | async-start | bytes 8192 | tf_op jit(solution)/shard_map/all_to_all | solution.py:126
  79.4 6.3 %all-to-all-done.2 = s32[8,2,1]{1,2,0:T(1,128)S(1)} async-done(((s32[8,2,1]{1,2,0:T(1,128)}), s32[8,2,1]{1,2,0:T(1,128)S(1)}, u32[]{:S(2)}, u32[]{:S(2)}) %all-to-all-start.2) | async-done | bytes 96 | tf_op jit(solution)/shard_map/all_to_all | solution.py:126
  86.6 5.0 %select_select_fusion = s32[2048]{0:T(1024)S(1)} fusion(pred[2048]{0:T(1024)(128)(4,1)S(1)} %copy-done.21, pred[2048]{0:T(1024)(128)(4,1)S(1)} %copy-done.20, pred[2048]{0:T(1024)(128)(4,1)S(1)} %copy-done.19, pred[2048]{0:T(1024)(128)(4,1)S(1)} %copy-done.18, pred[2048]{0:T(1024)(128)(4,1)S(1)} %copy-done.17, pred[2048]{0:T(1024)(128)(4,1)S(1)} %copy-done.16, ...), kind=kLoop, calls=%fused_computation.103 | loop fusion | flops 14336 | bytes 22560 | tf_op jit(solution)/shard_map/jit(_take)/gather | solution.py:46
  91.6 10.7 %all-gather.3.cloned.1.call-done = bf16[2048,768]{0,1:T(8,128)(2,1)} async-done(((bf16[2048,192]{0,1:T(8,128)(2,1)}), bf16[2048,768]{0,1:T(8,128)(2,1)}) %all-gather.3.cloned.1.call-update) | async-done | bytes 3145744 | tf_op jit(solution)/shard_map/all_gather | solution.py:133
  102.3 2.7 fusion.11
  105.1 1.1 convolution_convert_fusion.7
  106.3 1.1 convolution_convert_fusion.6
  107.5 1.1 convolution_convert_fusion.8
  108.6 25.0 %while.11 = (s32[]{:T(128)}, bf16[4,512,192]{1,2,0:T(8,128)(2,1)}, bf16[4,512,192]{1,2,0:T(8,128)(2,1)S(1)}, s32[4,512]{1,0:T(4,128)S(1)}, bf16[4,512,192]{1,2,0...) while((s32[]{:T(128)}, bf16[4,512,192]{1,2,0:T(8,128)(2,1)}, ...), condition=%wide.region_8.9_spmd, body=%wide.region_5.8_spmd.sunk | while | flops 206406144 | bytes 9193573 | solution.py:49
  109.0 3.0 fusion.111
  111.9 2.3 fusion.112
  115.2 3.0 fusion.111
  118.2 2.3 fusion.112
  121.4 3.0 fusion.111
  124.4 2.3 fusion.112
  127.7 3.0 fusion.111
  130.6 2.3 fusion.112
  133.6 1.2 copy.45
  134.9 2.7 convolution_convert_fusion.2
  137.6 38.0 %reduce-scatter.2.cloned.1.call-done = bf16[2048,192]{0,1:T(8,128)(2,1)} async-done(((bf16[2048,768]{0,1:T(8,128)(2,1)}), bf16[2048,192]{0,1:T(8,128)(2,1)}) %reduce-scatter.2.cloned.1.call-update) | async-done | bytes 786448 | tf_op jit(solution)/shard_map/reduce_scatter | solution.py:136
  175.6 2.3 add_convert_fusion
  178.2 28.4 %all-gather.5.cloned.1.call-done = bf16[2048,768]{0,1:T(8,128)(2,1)} async-done(((bf16[2048,192]{0,1:T(8,128)(2,1)}), bf16[2048,768]{0,1:T(8,128)(2,1)}) %all-gather.5.cloned.1.call-update) | async-done | bytes 3145744 | tf_op jit(solution)/shard_map/all_gather | solution.py:142
  206.6 2.7 fusion.14
  209.4 0.7 fusion.16
  210.6 0.8 convolution_convert_fusion.4
  211.7 0.8 fusion.46
  212.4 0.8 fusion.48
  213.7 0.8 fusion.21
  214.7 0.7 fusion.75
  215.4 1.8 fusion.25
  217.3 2.1 fusion.27
  219.4 1.8 fusion.26
  221.2 2.6 convolution_convert_fusion.5
  223.8 70.4 %all-reduce.3.cloned.1.call-done = (bf16[192,384]{1,0:T(8,128)(2,1)}, bf16[192,384]{1,0:T(8,128)(2,1)}, bf16[384,192]{0,1:T(8,128)(2,1)}) async-done(((bf16[192,384]{1,0:T(8,128)(2,1)}, bf16[192,384]{1,0:T(8,128)(2,1)}, bf16[384,192]{0,1:T(8,128)(2,1)}), (bf16[192,384]{1,0:T(8,128)(2,1)}, bf16[192,384]{1,0:T(8,128)(2,1)}, bf16[384,192]{0,1:T(8,128)(2,1)})) %all-reduce.3.cloned.1.call-update) | async-done | bytes 442384 | tf_op jit(solution)/shard_map/psum | solution.py:179
  294.2 1.4 fusion.30
  295.7 1.1 fusion.31
  296.8 3.8 %fusion.45 = f32[2048,384]{1,0:T(8,128)} fusion(bf16[2048,192]{0,1:T(8,128)(2,1)} %convolution_convert_fusion.5, bf16[192,384]{1,0:T(8,128)(2,1)} %get-tuple-element.94, f32[1,2,192,384]{3,2,1,0:T(8,128)} %param.24, f32[192]{0:T(256)S(1)} %add_rsqrt_fusion.4, f32[192]{0:T(256)S(1)} %sqrt.24), kind=kOutput, calls=%fused_computation.89 | convolution fusion | flops 302358528 | bytes 4376064 | tf_op jit(solution)/shard_map/dot_general | solution.py:189
  300.6 4.3 %fusion.18 = bf16[2048,192]{0,1:T(8,128)(2,1)} fusion(bf16[2048,192]{0,1:T(8,128)(2,1)S(1)} %copy-done.6, f32[2048,384]{1,0:T(8,128)} %fusion.45, bf16[2048,192]{0,1:T(8,128)(2,1)S(1)} %copy-done.7, bf16[192,384]{1,0:T(8,128)(2,1)S(1)} %copy-done.11, f32[1,2,192,384]{3,2,1,0:T(8,128)S(1)} %copy-done.4, bf16[384,192]{0,1:T(8,128)(2,1)S(1)} %copy-done.12, ...), kind=kOutput, calls=%fused_computation.39 | convolution fusion | flops 610615296 | bytes 6395904 | tf_op jit(solution)/shard_map/dot_general | solution.py:192
  (110 shorter events, 11.8 us)
Async XLA Ops:
  6.5 128.3 %copy-start = (bf16[192,768]{1,0:T(8,128)(2,1)S(1)}, bf16[192,768]{1,0:T(8,128)(2,1)}, u32[]{:S(2)}) copy-start(bf16[192,768]{1,0:T(8,128)(2,1)} %param.20) | copy-start | bytes 884740
  9.6 17.3 %all-to-all-start = ((s32[8,2,1]{1,2,0:T(1,128)}), s32[8,2,1]{1,2,0:T(1,128)S(1)}, u32[]{:S(2)}, u32[]{:S(2)}) async-start(s32[8,2,1]{1,2,0:T(1,128)} %bitcast.6), calls=%async_computation | async-start | bytes 8192 | tf_op jit(solution)/shard_map/all_to_all | solution.py:125
  26.9 42.4 %all-to-all-start.1 = ((bf16[8,2,49152]{2,1,0:T(2,128)(2,1)}), bf16[8,2,49152]{2,1,0:T(2,128)(2,1)S(1)}, u32[]{:S(2)}, u32[]{:S(2)}) async-start(bf16[8,2,49152]{2,1,0:T(2,128)(2,1)} %all_to_all.17), calls=%async_computation.1 | async-start | bytes 3145728 | tf_op jit(solution)/shard_map/all_to_all | solution.py:122
  32.9 69.4 %all-gather.3.cloned.1.call-start = ((), (), s32[]{:S(2)}) async-start(), calls=%async_computation.4 | async-start | bytes 3932160 | tf_op jit(solution)/shard_map/all_gather | solution.py:133
  69.9 16.6 %copy-start.15 = (pred[2048]{0:T(1024)(128)(4,1)S(1)}, pred[2048]{0:T(1024)(128)(4,1)}, u32[]{:S(2)}) copy-start(pred[2048]{0:T(1024)(128)(4,1)} %constant.200) | copy-start | bytes 6148
  70.0 16.6 %copy-start.16 = (pred[2048]{0:T(1024)(128)(4,1)S(1)}, pred[2048]{0:T(1024)(128)(4,1)}, u32[]{:S(2)}) copy-start(pred[2048]{0:T(1024)(128)(4,1)} %constant.199) | copy-start | bytes 6148
  70.0 16.6 %copy-start.17 = (pred[2048]{0:T(1024)(128)(4,1)S(1)}, pred[2048]{0:T(1024)(128)(4,1)}, u32[]{:S(2)}) copy-start(pred[2048]{0:T(1024)(128)(4,1)} %constant.198) | copy-start | bytes 6148
  70.0 16.6 %copy-start.18 = (pred[2048]{0:T(1024)(128)(4,1)S(1)}, pred[2048]{0:T(1024)(128)(4,1)}, u32[]{:S(2)}) copy-start(pred[2048]{0:T(1024)(128)(4,1)} %constant.197) | copy-start | bytes 6148
  70.0 16.6 %copy-start.19 = (pred[2048]{0:T(1024)(128)(4,1)S(1)}, pred[2048]{0:T(1024)(128)(4,1)}, u32[]{:S(2)}) copy-start(pred[2048]{0:T(1024)(128)(4,1)} %constant.196) | copy-start | bytes 6148
  70.0 16.6 %copy-start.20 = (pred[2048]{0:T(1024)(128)(4,1)S(1)}, pred[2048]{0:T(1024)(128)(4,1)}, u32[]{:S(2)}) copy-start(pred[2048]{0:T(1024)(128)(4,1)} %constant.195) | copy-start | bytes 6148
  70.0 16.6 %copy-start.21 = (pred[2048]{0:T(1024)(128)(4,1)S(1)}, pred[2048]{0:T(1024)(128)(4,1)}, u32[]{:S(2)}) copy-start(pred[2048]{0:T(1024)(128)(4,1)} %constant.194) | copy-start | bytes 6148
  73.6 31.4 %copy-start.22 = (bf16[3,768,192]{1,2,0:T(8,128)(2,1)S(1)}, bf16[3,768,192]{1,2,0:T(8,128)(2,1)}, u32[]{:S(2)}) copy-start(bf16[3,768,192]{1,2,0:T(8,128)(2,1)} %param.19) | copy-start | bytes 2654212
  73.6 31.4 %copy-start.23 = (f32[768]{0:T(1024)S(1)}, f32[768]{0:T(1024)}, u32[]{:S(2)}) copy-start(f32[768]{0:T(1024)} %param.18) | copy-start | bytes 9220
  75.5 10.1 %all-to-all-start.2 = ((s32[8,2,1]{1,2,0:T(1,128)}), s32[8,2,1]{1,2,0:T(1,128)S(1)}, u32[]{:S(2)}, u32[]{:S(2)}) async-start(s32[8,2,1]{1,2,0:T(1,128)} %bitcast.9), calls=%async_computation.2 | async-start | bytes 8192 | tf_op jit(solution)/shard_map/all_to_all | solution.py:126
  79.2 96.4 %reduce-scatter.2.cloned.1.call-start = ((), (), s32[]{:S(2)}) async-start(), calls=%async_computation.5 | async-start | bytes 3932160 | tf_op jit(solution)/shard_map/reduce_scatter | solution.py:136
  102.3 2.8 copy-start.5
  137.6 38.1 %copy-start.2 = (bf16[2048,192]{0,1:T(8,128)(2,1)S(1)}, bf16[2048,192]{0,1:T(8,128)(2,1)}, u32[]{:S(2)}) copy-start(bf16[2048,192]{0,1:T(8,128)(2,1)} %copy.34) | copy-start | bytes 2359300
  137.6 71.7 %copy-start.13 = (f32[768]{0:T(1024)S(1)}, f32[768]{0:T(1024)}, u32[]{:S(2)}) copy-start(f32[768]{0:T(1024)} %param.21) | copy-start | bytes 9220
  137.6 69.0 %all-gather.5.cloned.1.call-start = ((), (), s32[]{:S(2)}) async-start(), calls=%async_computation.6 | async-start | bytes 3932160 | tf_op jit(solution)/shard_map/all_gather | solution.py:142
  177.9 116.3 %all-reduce.3.cloned.1.call-start = ((), (), s32[]{:S(2)}) async-start(), calls=%async_computation.7 | async-start | bytes 884736 | tf_op jit(solution)/shard_map/psum | solution.py:179
  206.6 2.8 copy-start.1
  209.4 1.2 copy-start.10
  210.6 1.1 copy-start.3
  212.4 0.8 copy-start.14
  213.7 1.0 copy-start.8
  223.8 76.7 %copy-start.4 = (f32[1,2,192,384]{3,2,1,0:T(8,128)S(1)}, f32[1,2,192,384]{3,2,1,0:T(8,128)}, u32[]{:S(2)}) copy-start(f32[1,2,192,384]{3,2,1,0:T(8,128)} %param.24) | copy-start | bytes 1769476
  223.8 76.7 %copy-start.6 = (bf16[2048,192]{0,1:T(8,128)(2,1)S(1)}, bf16[2048,192]{0,1:T(8,128)(2,1)}, u32[]{:S(2)}) copy-start(bf16[2048,192]{0,1:T(8,128)(2,1)} %add_convert_fusion) | copy-start | bytes 2359300
  223.8 76.7 %copy-start.7 = (bf16[2048,192]{0,1:T(8,128)(2,1)S(1)}, bf16[2048,192]{0,1:T(8,128)(2,1)}, u32[]{:S(2)}) copy-start(bf16[2048,192]{0,1:T(8,128)(2,1)} %convolution_convert_fusion.5) | copy-start | bytes 2359300
  223.8 76.7 %copy-start.9 = (f32[1,384,192]{1,2,0:T(8,128)S(1)}, f32[1,384,192]{1,2,0:T(8,128)}, u32[]{:S(2)}) copy-start(f32[1,384,192]{1,2,0:T(8,128)} %param.25) | copy-start | bytes 884740
  294.2 6.3 %copy-start.11 = (bf16[192,384]{1,0:T(8,128)(2,1)S(1)}, bf16[192,384]{1,0:T(8,128)(2,1)}, u32[]{:S(2)}) copy-start(bf16[192,384]{1,0:T(8,128)(2,1)} %get-tuple-element.95) | copy-start | bytes 442372
  294.2 6.3 %copy-start.12 = (bf16[384,192]{0,1:T(8,128)(2,1)S(1)}, bf16[384,192]{0,1:T(8,128)(2,1)}, u32[]{:S(2)}) copy-start(bf16[384,192]{0,1:T(8,128)(2,1)} %get-tuple-element.96) | copy-start | bytes 442372
Sparse Core Ops, SparseCore 0:
  75.0 27.2 all-gather.2
  137.7 37.8 reduce-scatter.1
  178.1 28.4 all-gather.4
  221.3 72.8 all-reduce.2
where the time goes:
time: 312 us; the launch traced here: 311 us
  waiting for transfers between devices  190 us (61%)
  matrix products  50.9 us (16%)
  local copies, waits for them, and re-layouts  20.1 us (6%)
  other arithmetic  19.3 us (6%)
  starting transfers between devices  17.5 us (6%)
  between operations  13.5 us (4%)
    psum x1, waiting for transfers between devices, on_device(): lax.psum(grad_gate.astype(jnp.bfloat16), 'seq').astype(jnp.float32)  70.4 us
    reduce_scatter x1, waiting for transfers between devices, on_device(): lax.psum_scatter(partial_value.astype(jnp.bfloat16), 'head', scatter_dime...  38 us
    all_to_all x1, waiting for transfers between devices, on_device(): lax.all_to_all(pack_rows(selection, own_columns), 'seq', split_axis=0, co...  36.2 us
    all_gather x1, waiting for transfers between devices, on_device(): full_embedded = lax.all_gather(embedded, 'head', axis=1, tiled=True)  28.4 us
    sub x4, matrix products, attend_pair(): exp_scores = jnp.exp(scores - top_score)  11.9 us
    all_gather x1, waiting for transfers between devices, on_device(): lax.all_gather(view_own.reshape(BLK_DEV * BLK, width), 'head', axis=1, ti...  10.7 us
    dot_general x4, matrix products, attend_pair(): jnp.einsum('hqk,khe->qhe', weights, v_heads, preferred_element_type=jnp.f...  9.15 us
    all_to_all x1, starting transfers between devices, on_device(): lax.all_to_all(sent_dest, 'seq', split_axis=0, concat_axis=0, tiled=True)  7.28 us
  transfers between devices with their start and end apart: 7, of which 6 were waited for; matrix products, arithmetic and copies ran while one was open for 6% of the time, Pallas kernels for 0%

commit v1 on v0

--- a/solution.py
+++ b/solution.py
@@ -176,7 +176,7 @@
     grad_gate = jnp.einsum("tf,th->fh", fast_key, gate_grad, preferred_element_type=jnp.float32)
     grad_up = jnp.einsum("tf,th->fh", fast_key, up_grad, preferred_element_type=jnp.float32)
     grad_gate, grad_up, grad_down = (
-        lax.psum(grad_gate.astype(jnp.bfloat16), "seq").astype(jnp.float32),
+        jnp.sum(lax.all_gather(grad_gate.astype(jnp.bfloat16), "seq"), axis=0).astype(jnp.float32),
         lax.psum(grad_up.astype(jnp.bfloat16), "seq").astype(jnp.float32),
         lax.psum(grad_down.astype(jnp.bfloat16), "seq").astype(jnp.float32),
     )

time: 312 us -> 351 us (1.12)
  waiting for transfers between devices: 190 us -> 223 us
  matrix products: 50.9 us -> 54.5 us
    all_gather x0 -> x1, waiting for transfers between devices: none -> 41.1 us  [on_device(): lax.all_gather(grad_gate.astype(jnp.bfloat16), 'seq')]
    psum x1, waiting for transfers between devices: 70.4 us -> 62.8 us  [on_device(): lax.psum(grad_up.astype(jnp.bfloat16), 'seq').astype(jnp.float32)]
    dot_general x1, matrix products: 2.13 us -> 6.09 us  [on_device(): jnp.einsum('tf,th->fh', fast_key, gate_grad, preferred_element_type=jnp.f...]
  transfers between devices with their start and end apart: 7 -> 8, of which waited for: 6 -> 7; matrix products, arithmetic and copies ran while one was open for 6% -> 7% of each run, Pallas kernels for 0% -> 0%
where the time goes in v1:
time: 351 us; the launch traced here: 350 us
  waiting for transfers between devices  223 us (64%)
  matrix products  54.5 us (16%)
  other arithmetic  20.8 us (6%)
  local copies, waits for them, and re-layouts  20.3 us (6%)
  starting transfers between devices  17.5 us (5%)
  between operations  13.6 us (4%)
    psum x1, waiting for transfers between devices, on_device(): lax.psum(grad_up.astype(jnp.bfloat16), 'seq').astype(jnp.float32)  62.8 us
    all_gather x1, waiting for transfers between devices, on_device(): lax.all_gather(grad_gate.astype(jnp.bfloat16), 'seq')  41.1 us
    reduce_scatter x1, waiting for transfers between devices, on_device(): lax.psum_scatter(partial_value.astype(jnp.bfloat16), 'head', scatter_dime...  38 us
    all_to_all x1, waiting for transfers between devices, on_device(): lax.all_to_all(pack_rows(selection, own_columns), 'seq', split_axis=0, co...  36.2 us
    all_gather x1, waiting for transfers between devices, on_device(): full_embedded = lax.all_gather(embedded, 'head', axis=1, tiled=True)  28.4 us
    sub x4, matrix products, attend_pair(): exp_scores = jnp.exp(scores - top_score)  11.8 us
    all_gather x1, waiting for transfers between devices, on_device(): lax.all_gather(view_own.reshape(BLK_DEV * BLK, width), 'head', axis=1, ti...  10.7 us
    dot_general x4, matrix products, attend_pair(): jnp.einsum('hqk,khe->qhe', weights, v_heads, preferred_element_type=jnp.f...  9.14 us
  transfers between devices with their start and end apart: 8, of which 7 were waited for; matrix products, arithmetic and copies ran while one was open for 7% of the time, Pallas kernels for 0%

profile of v1, /device:TPU:0, one launch (start us, length us, event | category | flops | bytes accessed | tf_op | source)
XLA Modules:
  0.0 350.4 jit_solution(12756844559185382576)
XLA Ops:
  9.6 7.3 %all-to-all-start = ((s32[8,2,1]{1,2,0:T(1,128)}), s32[8,2,1]{1,2,0:T(1,128)S(1)}, u32[]{:S(2)}, u32[]{:S(2)}) async-start(s32[8,2,1]{1,2,0:T(1,128)} %bitcast.6), calls=%async_computation | async-start | bytes 8192 | tf_op jit(solution)/shard_map/all_to_all | solution.py:125
  16.8 2.9 constant_dynamic-slice_fusion.4
  19.8 3.2 reshape.274
  23.0 2.0 convolution_convert_fusion
  24.9 1.9 all_to_all.17
  26.9 6.0 %all-to-all-start.1 = ((bf16[8,2,49152]{2,1,0:T(2,128)(2,1)}), bf16[8,2,49152]{2,1,0:T(2,128)(2,1)S(1)}, u32[]{:S(2)}, u32[]{:S(2)}) async-start(bf16[8,2,49152]{2,1,0:T(2,128)(2,1)} %all_to_all.17), calls=%async_computation.1 | async-start | bytes 3145728 | tf_op jit(solution)/shard_map/all_to_all | solution.py:122
  33.1 36.2 %all-to-all-done.1 = bf16[8,2,49152]{2,1,0:T(2,128)(2,1)S(1)} async-done(((bf16[8,2,49152]{2,1,0:T(2,128)(2,1)}), bf16[8,2,49152]{2,1,0:T(2,128)(2,1)S(1)}, u32[]{:S(2)}, u32[]{:S(2)}) %all-to-all-start.1) | async-done | bytes 1572896 | tf_op jit(solution)/shard_map/all_to_all | solution.py:122
  70.0 1.2 convolution_convert_fusion.1
  71.3 2.3 reshape.275
  73.6 1.2 copy.34
  75.5 3.6 %all-to-all-start.2 = ((s32[8,2,1]{1,2,0:T(1,128)}), s32[8,2,1]{1,2,0:T(1,128)S(1)}, u32[]{:S(2)}, u32[]{:S(2)}) async-start(s32[8,2,1]{1,2,0:T(1,128)} %bitcast.9), calls=%async_computation.2 | async-start | bytes 8192 | tf_op jit(solution)/shard_map/all_to_all | solution.py:126
  79.4 6.3 %all-to-all-done.2 = s32[8,2,1]{1,2,0:T(1,128)S(1)} async-done(((s32[8,2,1]{1,2,0:T(1,128)}), s32[8,2,1]{1,2,0:T(1,128)S(1)}, u32[]{:S(2)}, u32[]{:S(2)}) %all-to-all-start.2) | async-done | bytes 96 | tf_op jit(solution)/shard_map/all_to_all | solution.py:126
  86.6 5.0 %select_select_fusion = s32[2048]{0:T(1024)S(1)} fusion(pred[2048]{0:T(1024)(128)(4,1)S(1)} %copy-done.25, pred[2048]{0:T(1024)(128)(4,1)S(1)} %copy-done.24, pred[2048]{0:T(1024)(128)(4,1)S(1)} %copy-done.23, pred[2048]{0:T(1024)(128)(4,1)S(1)} %copy-done.22, pred[2048]{0:T(1024)(128)(4,1)S(1)} %copy-done.21, pred[2048]{0:T(1024)(128)(4,1)S(1)} %copy-done.20, ...), kind=kLoop, calls=%fused_computation.103 | loop fusion | flops 14336 | bytes 22560 | tf_op jit(solution)/shard_map/jit(_take)/gather | solution.py:46
  91.6 10.7 %all-gather.5.cloned.1.call-done = bf16[2048,768]{0,1:T(8,128)(2,1)} async-done(((bf16[2048,192]{0,1:T(8,128)(2,1)}), bf16[2048,768]{0,1:T(8,128)(2,1)}) %all-gather.5.cloned.1.call-update) | async-done | bytes 3145744 | tf_op jit(solution)/shard_map/all_gather | solution.py:133
  102.3 2.7 fusion.11
  105.1 1.1 convolution_convert_fusion.7
  106.3 1.1 convolution_convert_fusion.6
  107.5 1.1 convolution_convert_fusion.8
  108.6 25.0 %while.11 = (s32[]{:T(128)}, bf16[4,512,192]{1,2,0:T(8,128)(2,1)}, bf16[4,512,192]{1,2,0:T(8,128)(2,1)S(1)}, s32[4,512]{1,0:T(4,128)S(1)}, bf16[4,512,192]{1,2,0...) while((s32[]{:T(128)}, bf16[4,512,192]{1,2,0:T(8,128)(2,1)}, ...), condition=%wide.region_8.9_spmd, body=%wide.region_5.8_spmd.sunk | while | flops 206406144 | bytes 9193573 | solution.py:49
  108.9 3.0 fusion.111
  111.9 2.3 fusion.112
  115.2 3.0 fusion.111
  118.2 2.3 fusion.112
  121.5 3.0 fusion.111
  124.4 2.3 fusion.112
  127.7 3.0 fusion.111
  130.6 2.3 fusion.112
  133.6 1.2 copy.45
  134.9 2.7 convolution_convert_fusion.2
  137.6 38.0 %reduce-scatter.2.cloned.1.call-done = bf16[2048,192]{0,1:T(8,128)(2,1)} async-done(((bf16[2048,768]{0,1:T(8,128)(2,1)}), bf16[2048,192]{0,1:T(8,128)(2,1)}) %reduce-scatter.2.cloned.1.call-update) | async-done | bytes 786448 | tf_op jit(solution)/shard_map/reduce_scatter | solution.py:136
  175.6 2.3 add_convert_fusion
  178.2 28.4 %all-gather.7.cloned.1.call-done = bf16[2048,768]{0,1:T(8,128)(2,1)} async-done(((bf16[2048,192]{0,1:T(8,128)(2,1)}), bf16[2048,768]{0,1:T(8,128)(2,1)}) %all-gather.7.cloned.1.call-update) | async-done | bytes 3145744 | tf_op jit(solution)/shard_map/all_gather | solution.py:142
  206.6 2.7 fusion.14
  210.6 0.8 convolution_convert_fusion.4
  211.7 0.8 fusion.46
  213.8 0.8 fusion.21
  214.9 0.8 fusion.75
  215.7 1.8 fusion.25
  217.5 1.8 fusion.26
  219.4 6.1 %fusion.27 = bf16[192,384]{1,0:T(8,128)(2,1)} fusion(bf16[2048,192]{0,1:T(8,128)(2,1)} %copy-done.2, f32[2048,384]{1,0:T(8,128)} %copy-done.7, f32[2048,384]{1,0:T(8,128)} %copy-done.9, f32[2048,384]{1,0:T(8,128)} %copy-done.8), kind=kOutput, calls=%fused_computation.55 | convolution fusion | flops 309927936 | bytes 10371072 | tf_op jit(solution)/shard_map/tf,th->fh/dot_general | solution.py:176
  225.5 2.7 convolution_convert_fusion.5
  228.2 62.8 %all-reduce.3.cloned.1.call-done = (bf16[192,384]{1,0:T(8,128)(2,1)}, bf16[384,192]{0,1:T(8,128)(2,1)}) async-done(((bf16[192,384]{1,0:T(8,128)(2,1)}, bf16[384,192]{0,1:T(8,128)(2,1)}), (bf16[192,384]{1,0:T(8,128)(2,1)}, bf16[384,192]{0,1:T(8,128)(2,1)})) %all-reduce.3.cloned.1.call-update) | async-done | bytes 294928 | tf_op jit(solution)/shard_map/psum | solution.py:180
  290.9 1.1 fusion.31
  292.0 41.1 %all-gather.9.cloned.1.call-done = bf16[1536,384]{1,0:T(8,128)(2,1)} async-done(((bf16[192,384]{1,0:T(8,128)(2,1)}), bf16[1536,384]{1,0:T(8,128)(2,1)}) %all-gather.9.cloned.1.call-update) | async-done | bytes 1179664 | tf_op jit(solution)/shard_map/all_gather | solution.py:179
  333.2 1.6 reduce_sum.135
  334.7 1.3 fusion.30
  336.1 3.4 fusion.45
  339.6 4.3 %fusion.18 = bf16[2048,192]{0,1:T(8,128)(2,1)} fusion(bf16[2048,192]{0,1:T(8,128)(2,1)S(1)} %copy-done.10, f32[2048,384]{1,0:T(8,128)} %fusion.45, bf16[2048,192]{0,1:T(8,128)(2,1)S(1)} %copy-done.11, bf16[192,384]{1,0:T(8,128)(2,1)S(1)} %copy-done.15, f32[1,2,192,384]{3,2,1,0:T(8,128)S(1)} %copy-done.5, bf16[384,192]{0,1:T(8,128)(2,1)S(1)} %copy-done.16, ...), kind=kOutput, calls=%fused_computation.39 | convolution fusion | flops 610615296 | bytes 6395904 | tf_op jit(solution)/shard_map/dot_general | solution.py:192
  (122 shorter events, 13.6 us)
Async XLA Ops:
  6.5 128.3 %copy-start = (bf16[192,768]{1,0:T(8,128)(2,1)S(1)}, bf16[192,768]{1,0:T(8,128)(2,1)}, u32[]{:S(2)}) copy-start(bf16[192,768]{1,0:T(8,128)(2,1)} %param.20) | copy-start | bytes 884740
  9.6 17.3 %all-to-all-start = ((s32[8,2,1]{1,2,0:T(1,128)}), s32[8,2,1]{1,2,0:T(1,128)S(1)}, u32[]{:S(2)}, u32[]{:S(2)}) async-start(s32[8,2,1]{1,2,0:T(1,128)} %bitcast.6), calls=%async_computation | async-start | bytes 8192 | tf_op jit(solution)/shard_map/all_to_all | solution.py:125
  26.9 42.4 %all-to-all-start.1 = ((bf16[8,2,49152]{2,1,0:T(2,128)(2,1)}), bf16[8,2,49152]{2,1,0:T(2,128)(2,1)S(1)}, u32[]{:S(2)}, u32[]{:S(2)}) async-start(bf16[8,2,49152]{2,1,0:T(2,128)(2,1)} %all_to_all.17), calls=%async_computation.1 | async-start | bytes 3145728 | tf_op jit(solution)/shard_map/all_to_all | solution.py:122
  32.9 69.4 %all-gather.5.cloned.1.call-start = ((), (), s32[]{:S(2)}) async-start(), calls=%async_computation.4 | async-start | bytes 3932160 | tf_op jit(solution)/shard_map/all_gather | solution.py:133
  69.9 16.6 %copy-start.19 = (pred[2048]{0:T(1024)(128)(4,1)S(1)}, pred[2048]{0:T(1024)(128)(4,1)}, u32[]{:S(2)}) copy-start(pred[2048]{0:T(1024)(128)(4,1)} %constant.201) | copy-start | bytes 6148
  69.9 16.6 %copy-start.20 = (pred[2048]{0:T(1024)(128)(4,1)S(1)}, pred[2048]{0:T(1024)(128)(4,1)}, u32[]{:S(2)}) copy-start(pred[2048]{0:T(1024)(128)(4,1)} %constant.200) | copy-start | bytes 6148
  70.0 16.6 %copy-start.21 = (pred[2048]{0:T(1024)(128)(4,1)S(1)}, pred[2048]{0:T(1024)(128)(4,1)}, u32[]{:S(2)}) copy-start(pred[2048]{0:T(1024)(128)(4,1)} %constant.199) | copy-start | bytes 6148
  70.0 16.6 %copy-start.22 = (pred[2048]{0:T(1024)(128)(4,1)S(1)}, pred[2048]{0:T(1024)(128)(4,1)}, u32[]{:S(2)}) copy-start(pred[2048]{0:T(1024)(128)(4,1)} %constant.198) | copy-start | bytes 6148
  70.0 16.6 %copy-start.23 = (pred[2048]{0:T(1024)(128)(4,1)S(1)}, pred[2048]{0:T(1024)(128)(4,1)}, u32[]{:S(2)}) copy-start(pred[2048]{0:T(1024)(128)(4,1)} %constant.197) | copy-start | bytes 6148
  70.0 16.6 %copy-start.24 = (pred[2048]{0:T(1024)(128)(4,1)S(1)}, pred[2048]{0:T(1024)(128)(4,1)}, u32[]{:S(2)}) copy-start(pred[2048]{0:T(1024)(128)(4,1)} %constant.196) | copy-start | bytes 6148
  70.0 16.6 %copy-start.25 = (pred[2048]{0:T(1024)(128)(4,1)S(1)}, pred[2048]{0:T(1024)(128)(4,1)}, u32[]{:S(2)}) copy-start(pred[2048]{0:T(1024)(128)(4,1)} %constant.195) | copy-start | bytes 6148
  73.6 31.4 %copy-start.26 = (bf16[3,768,192]{1,2,0:T(8,128)(2,1)S(1)}, bf16[3,768,192]{1,2,0:T(8,128)(2,1)}, u32[]{:S(2)}) copy-start(bf16[3,768,192]{1,2,0:T(8,128)(2,1)} %param.19) | copy-start | bytes 2654212
  73.6 31.4 %copy-start.27 = (f32[768]{0:T(1024)S(1)}, f32[768]{0:T(1024)}, u32[]{:S(2)}) copy-start(f32[768]{0:T(1024)} %param.18) | copy-start | bytes 9220
  75.5 10.1 %all-to-all-start.2 = ((s32[8,2,1]{1,2,0:T(1,128)}), s32[8,2,1]{1,2,0:T(1,128)S(1)}, u32[]{:S(2)}, u32[]{:S(2)}) async-start(s32[8,2,1]{1,2,0:T(1,128)} %bitcast.9), calls=%async_computation.2 | async-start | bytes 8192 | tf_op jit(solution)/shard_map/all_to_all | solution.py:126
  79.2 96.4 %reduce-scatter.2.cloned.1.call-start = ((), (), s32[]{:S(2)}) async-start(), calls=%async_computation.5 | async-start | bytes 3932160 | tf_op jit(solution)/shard_map/reduce_scatter | solution.py:136
  102.3 2.8 copy-start.6
  137.6 38.1 %copy-start.3 = (bf16[2048,192]{0,1:T(8,128)(2,1)S(1)}, bf16[2048,192]{0,1:T(8,128)(2,1)}, u32[]{:S(2)}) copy-start(bf16[2048,192]{0,1:T(8,128)(2,1)} %copy.34) | copy-start | bytes 2359300
  137.6 71.7 %copy-start.17 = (f32[768]{0:T(1024)S(1)}, f32[768]{0:T(1024)}, u32[]{:S(2)}) copy-start(f32[768]{0:T(1024)} %param.21) | copy-start | bytes 9220
  137.6 69.0 %all-gather.7.cloned.1.call-start = ((), (), s32[]{:S(2)}) async-start(), calls=%async_computation.6 | async-start | bytes 3932160 | tf_op jit(solution)/shard_map/all_gather | solution.py:142
  177.9 113.0 %all-reduce.3.cloned.1.call-start = ((), (), s32[]{:S(2)}) async-start(), calls=%async_computation.8 | async-start | bytes 589824 | tf_op jit(solution)/shard_map/psum | solution.py:180
  206.6 2.8 copy-start.1
  209.4 1.2 copy-start.14
  210.6 1.1 copy-start.4
  211.7 5.8 %copy-start.2 = (bf16[2048,192]{0,1:T(8,128)(2,1)}, bf16[2048,192]{0,1:T(8,128)(2,1)S(1)}, u32[]{:S(2)}) copy-start(bf16[2048,192]{0,1:T(8,128)(2,1)S(1)} %convolution_convert_fusion.4) | copy-start | bytes 2359300
  212.4 5.1 %copy-start.7 = (f32[2048,384]{1,0:T(8,128)}, f32[2048,384]{1,0:T(8,128)S(1)}, u32[]{:S(2)}) copy-start(f32[2048,384]{1,0:T(8,128)S(1)} %fusion.46) | copy-start | bytes 9437188
  212.4 0.8 copy-start.18
  213.2 2.5 copy-start.8
  213.7 1.2 copy-start.12
  215.7 1.8 copy-start.9
  219.3 113.8 %all-gather.9.cloned.1.call-start = ((), (), s32[]{:S(2)}) async-start(), calls=%async_computation.7 | async-start | bytes 1327104 | tf_op jit(solution)/shard_map/all_gather | solution.py:179
  228.2 108.0 %copy-start.11 = (bf16[2048,192]{0,1:T(8,128)(2,1)S(1)}, bf16[2048,192]{0,1:T(8,128)(2,1)}, u32[]{:S(2)}) copy-start(bf16[2048,192]{0,1:T(8,128)(2,1)} %convolution_convert_fusion.5) | copy-start | bytes 2359300
  333.2 6.4 %copy-start.5 = (f32[1,2,192,384]{3,2,1,0:T(8,128)S(1)}, f32[1,2,192,384]{3,2,1,0:T(8,128)}, u32[]{:S(2)}) copy-start(f32[1,2,192,384]{3,2,1,0:T(8,128)} %param.24) | copy-start | bytes 1769476
  333.2 6.4 %copy-start.10 = (bf16[2048,192]{0,1:T(8,128)(2,1)S(1)}, bf16[2048,192]{0,1:T(8,128)(2,1)}, u32[]{:S(2)}) copy-start(bf16[2048,192]{0,1:T(8,128)(2,1)} %add_convert_fusion) | copy-start | bytes 2359300
  333.2 6.4 %copy-start.13 = (f32[1,384,192]{1,2,0:T(8,128)S(1)}, f32[1,384,192]{1,2,0:T(8,128)}, u32[]{:S(2)}) copy-start(f32[1,384,192]{1,2,0:T(8,128)} %param.25) | copy-start | bytes 884740
  333.2 6.4 %copy-start.15 = (bf16[192,384]{1,0:T(8,128)(2,1)S(1)}, bf16[192,384]{1,0:T(8,128)(2,1)}, u32[]{:S(2)}) copy-start(bf16[192,384]{1,0:T(8,128)(2,1)} %get-tuple-element.94) | copy-start | bytes 442372
  333.2 6.4 %copy-start.16 = (bf16[384,192]{0,1:T(8,128)(2,1)S(1)}, bf16[384,192]{0,1:T(8,128)(2,1)}, u32[]{:S(2)}) copy-start(bf16[384,192]{0,1:T(8,128)(2,1)} %get-tuple-element.95) | copy-start | bytes 442372
Sparse Core Ops, SparseCore 0:
  75.0 27.2 all-gather.4
  137.7 37.8 reduce-scatter.1
  178.1 28.4 all-gather.6
  219.4 71.4 all-reduce.2
  292.9 40.1 all-gather.8
